TPU v7x, 32 devices: a whole 2x2x4 slice. The times are simulated.
32 devices in a mesh: member: 2 (over x), lon: 8 (over z, y), lat: 2 (over core).
Axes of the slice: x: 2, y: 2, z: 4, core: 2. Of those that a mesh axis runs over, the one named last changes fastest.
Arguments:
- strain_rate: float32 [3, 256, 2160], P(None, 'lon', 'lat'), may hold values from -6 to 6
- stress_start: float32 [3, 256, 2160], P(None, 'lon', 'lat'), may hold values from -3 to 3
- concentration: float32 [256, 2160], P('lon', 'lat'), may hold values from 0.5 to 1
- cell_class: int32 [512, 2160], P(('member', 'lon'), 'lat'), parts along dimension 0, may hold values from 0 to 7
- land_mask: int32 [256, 2160], P('lon', 'lat'), may hold values 0 or 1
- fold_partner: int32 [256], replicated, may hold values from 0 to 255, each once
- kernel_weights: float32 [7, 7], replicated, may hold values from 0.05 to 0.5
Outputs:
- stress_out: float32 [3, 512, 2160], P(None, ('member', 'lon'), 'lat'), parts along dimension 1
- damage_out: float32 [512, 2160], P(('member', 'lon'), 'lat'), parts along dimension 0
- mean_overstress: float32 [6], P('member'), parts along dimension 0
There are 2 independent parts, one for each index of `member`. A program takes and returns all parts, laid end to end along the dimension named above; an argument that names none is the same for every part. Nothing has to cross between parts.
Inputs may be any that keep to these rules, and one draw needn't show every extreme that they name: `fold_partner`: each of the 256 longitude indices appears once.
All inputs are finite; a program needn't handle non-finite values. No bound on the sum of `land_mask` on one device may be relied on, other than what follows from the above.
Results may differ from a plain program's by a relative error of at most 0.0001.
Values sent between devices are 32-bit elements; how exact they have to be, the bound alone decides.
A program may use at most 64 MiB of HBM per device.

v0:
```python
import jax
import jax.numpy as jnp
from jax import lax
from jax.sharding import PartitionSpec as P

ITERS = 3


def padded_2(array, sides, width):
    for axis, dim in sides:
        size, length = (lax.axis_size(axis), array.shape[dim])
        up = [(i, (i + 1) % size) for i in range(size)]
        down = [(j, i) for i, j in up]
        last = lax.slice_in_dim(array, length - width, length, axis=dim)
        first = lax.slice_in_dim(array, 0, width, axis=dim)
        before = lax.ppermute(last, axis, up)
        after = lax.ppermute(first, axis, down)
        array = jnp.concatenate([before, array, after], axis=dim)
    return array


def smooth(padded, weights, ncols, nrows):
    side = weights.shape[0]
    total = jnp.zeros((padded.shape[0], ncols, nrows), jnp.float32)
    for first in range(side):
        for second in range(side):
            total = (
                total
                + weights[first, second] * padded[:, first : first + ncols, second : second + nrows]
            )
    return total


def extend(fields, partner, width):
    ncols = fields.shape[1]
    top = jnp.swapaxes(fields[:, :, -width:], 1, 2)
    whole_top = lax.all_gather(top, "lon", axis=2, tiled=True)
    total_cols = whole_top.shape[2]
    first_col = lax.axis_index("lon") * ncols
    columns = (first_col - width + jnp.arange(ncols + 2 * width, dtype=jnp.int32)) % total_cols
    picked = jnp.take(partner, columns)
    rows = jnp.take(whole_top, picked, axis=2)
    north = jnp.swapaxes(rows[:, ::-1, :], 1, 2)
    lat_place = lax.axis_index("lat")
    lat_last = lax.axis_size("lat") - 1
    padded = padded_2(fields, (("lon", 1), ("lat", 2)), width)
    south_rim = jnp.where(
        lat_place == 0, jnp.zeros_like(padded[:, :, :width]), padded[:, :, :width]
    )
    north_rim = jnp.where(lat_place == lat_last, north, padded[:, :, -width:])
    return jnp.concatenate([south_rim, padded[:, :, width:-width], north_rim], axis=2)


def ocean_excess(local_excess, count):
    excess, ocean_total = lax.psum((local_excess, count), ("lon", "lat"))
    return excess / (ocean_total + 1.0)


def shards(
    strain_rate, stress_start, concentration, cell_class, land_mask, fold_partner, kernel_weights
):
    width = kernel_weights.shape[0] // 2
    ocean = land_mask.astype(jnp.float32)
    ncols, nrows = ocean.shape
    denom = smooth(extend(ocean[None], fold_partner, width), kernel_weights, ncols, nrows)[0] + 1.0
    count = jnp.sum(ocean)
    damage = ocean * 0.1 * cell_class.astype(jnp.float32) * concentration
    stress = ocean[None] * stress_start
    base = concentration * jnp.exp(-2.0 * (1.0 - concentration))
    e_one, e_two, e_shear = (strain_rate[0], strain_rate[1], strain_rate[2])
    load = jnp.stack([e_one + e_two / 3.0, e_two + e_one / 3.0, e_shear / (4.0 / 3.0)]) / (
        8.0 / 9.0
    )
    means = []
    for step in range(ITERS):
        keep = 1.0 - damage
        theta = 0.5 / (keep * keep)
        elastic = ocean[None] * (stress + (base * keep)[None] * load) / (1.0 + theta)[None]
        half_diff = (elastic[0] - elastic[1]) / 2.0
        tau = jnp.sqrt(half_diff * half_diff + elastic[2] * elastic[2] + 0.25)
        ratio = (tau + 0.7 * (elastic[0] + elastic[1]) / 2.0) / (0.6 * concentration)
        over = jnp.maximum(ratio, 1.0)
        q_part = 1.0 - 1.0 / over
        local_excess = jnp.sum(ocean * (over - 1.0))
        mean_now = ocean_excess(local_excess, count)
        factor = 1.0 / (1.0 + 2.0 * mean_now)
        local_damage = ocean * (damage + factor * keep * q_part)
        local_stress = elastic * (1.0 - factor * q_part)[None]
        fields = jnp.concatenate([local_damage[None], local_stress], axis=0)
        averaged = (
            smooth(extend(fields, fold_partner, width), kernel_weights, ncols, nrows) / denom[None]
        )
        fresh = ocean[None] * (0.5 * fields + 0.5 * averaged)
        means.append(mean_now)
        damage = fresh[0]
        stress = fresh[1:]
    return (stress, damage, jnp.stack(means))


def solution(mesh):
    in_specs = (
        P(None, "lon", "lat"),
        P(None, "lon", "lat"),
        P("lon", "lat"),
        P(("member", "lon"), "lat"),
        P("lon", "lat"),
        P(),
        P(),
    )
    out_specs = (P(None, ("member", "lon"), "lat"), P(("member", "lon"), "lat"), P("member"))
    return jax.shard_map(shards, mesh=mesh, in_specs=in_specs, out_specs=out_specs, check_vma=False)
```

profile of v0, /device:TPU:1, one launch (start us, length us, event | category | flops | bytes accessed | tf_op | source)
XLA Modules:
  0.0 402.6 jit_solution(4473305265631229765)
XLA Ops:
  0.7 1.0 convert_bitcast_fusion
  1.7 2.1 collective-permute-start.4
  3.8 3.1 collective-permute-start.5
  7.1 0.9 copy-done.3
  8.1 0.7 convert_reduce_fusion
  8.8 30.4 %all-reduce = (f32[]{:T(128)}, f32[]{:T(128)}) all-reduce(f32[]{:T(128)} %get-tuple-element.12, f32[]{:T(128)} %get-tuple-element.11), channel_id=1, replica_groups=mesh['member'=2,'lon'=8,'lat'=2] {'lon','lat'}, use_global_device_ids=true, to_apply=%region_1.2 | all-reduce | flops 2 | bytes 16 | tf_op jit(solution)/shard_map/psum | solution.py:55
  40.9 4.1 %collective-permute-start.1 = (f32[4,3,1080]{2,1,0:T(4,128)S(1)}, f32[4,3,1080]{2,1,0:T(4,128)S(1)}, u32[]{:S(2)}, u32[]{:S(2)}) collective-permute-start(f32[4,3,1080]{2,1,0:T(4,128)S(1)} %get-tuple-element.45), channel_id=1, source_target_pairs={{2,0},{4,2},{6,4},{8,6},{10,8},{12,10},{14,12},{0,14},{3,1},{5,3},... | collective-permute-start | bytes 155528 | tf_op jit(solution)/shard_map/ppermute | solution.py:17
  45.1 0.7 fusion.262
  45.8 0.7 fusion.263
  46.7 0.8 gather_fusion.1
  47.5 24.3 %all_gather.13 = f32[1,3,256]{1,2,0:T(8,128)S(1)} all-gather(f32[1,3,32]{1,2,0:T(8,128)S(1)} %slice_bitcast_fusion.1), channel_id=1, replica_groups=mesh['member'=2,'lon'=8,'lat'=2] {'lon'}, dimensions={2}, use_global_device_ids=true | all-gather | bytes 3456 | tf_op jit(solution)/shard_map/all_gather | solution.py:37
  71.9 24.9 %all_gather.12 = f32[4,3,256]{1,0,2:T(4,128)S(1)} all-gather(f32[4,3,32]{1,0,2:T(4,128)S(1)} %copy.60), channel_id=1, replica_groups=mesh['member'=2,'lon'=8,'lat'=2] {'lon'}, dimensions={2}, use_global_device_ids=true | all-gather | bytes 13824 | tf_op jit(solution)/shard_map/all_gather | solution.py:37
  96.8 0.6 gather_fusion
  97.4 0.6 gather_fusion.2
  98.1 0.7 fusion.264
  98.9 14.5 %collective-permute-start.6 = (f32[1,38,3]{2,1,0:T(8,128)S(1)}, f32[1,38,3]{2,1,0:T(8,128)S(1)}, u32[]{:S(2)}, u32[]{:S(2)}) collective-permute-start(f32[1,38,3]{2,1,0:T(8,128)S(1)} %get-tuple-element.53), channel_id=1, source_target_pairs={{0,1},{1,0},{2,3},{3,2},{4,5},{5,4},{6,7},{7,6},{8,9},{9,8},{10,11... | collective-permute-start | bytes 1376 | tf_op jit(solution)/shard_map/ppermute | solution.py:16
  113.7 0.6 collective-permute-done.6
  114.3 0.6 collective-permute-done.7
  115.0 31.9 %fusion.171 = f32[32,1080]{1,0:T(8,128)S(1)} fusion(f32[1,32,1080]{2,1,0:T(8,128)S(1)} %get-tuple-element.61, f32[1,3,1080]{2,1,0:T(4,128)S(1)} %collective-permute-done.5, f32[1,3,1080]{2,1,0:T(4,128)S(1)} %collective-permute-done.4, f32[1,38,1083]{2,1,0:T(8,128)S(1)} %get-tuple-element.52, f32[1,38,1083]{2,1,0:T(8,128)S(1)} %get-tuple-element.51, ...), kind=kLoop, calls=%fused_computation.370 | loop fusion | flops 3628800 | bytes 6246916 | tf_op jit(solution)/shard_map/div | solution.py:91
  147.0 0.2 collective-permute-start.2
  147.3 0.3 collective-permute-start.3
  147.7 0.7 collective-permute-done.2
  148.4 0.2 collective-permute-done.3
  148.5 0.4 maximum_maximum_fusion
  148.9 36.4 %fusion.105 = f32[4,32,1080]{2,1,0:T(8,128)S(1)} fusion(f32[4,38,1083]{2,1,0:T(8,128)S(1)} %get-tuple-element.31, f32[4,35,1080]{2,1,0:T(8,128)S(1)} %get-tuple-element.43, f32[4,38,1083]{2,1,0:T(8,128)S(1)} %get-tuple-element.30, f32[4,35,1080]{2,1,0:T(8,128)S(1)} %get-tuple-element.42, f32[3,32,1080]{2,1,0:T(8,128)S(1)} %broadcast_multiply_fusion.2, ...), kind=kLoop, calls=%fused_computation.240 | loop fusion | flops 13962240 | bytes 27924676 | tf_op jit(solution)/shard_map/mul | solution.py:93
  185.5 0.7 multiply_reduce_fusion.1
  186.2 29.8 %psum.36 = f32[]{:T(128)} all-reduce(f32[]{:T(128)} %get-tuple-element.17), channel_id=1, replica_groups=mesh['member'=2,'lon'=8,'lat'=2] {'lon','lat'}, use_global_device_ids=true, to_apply=%region_5.8 | all-reduce | flops 1 | bytes 8 | tf_op jit(solution)/shard_map/psum | solution.py:55
  217.1 4.1 %collective-permute-start.9 = (f32[4,3,1080]{2,1,0:T(4,128)S(1)}, f32[4,3,1080]{2,1,0:T(4,128)S(1)}, u32[]{:S(2)}, u32[]{:S(2)}) collective-permute-start(f32[4,3,1080]{2,1,0:T(4,128)S(1)} %get-tuple-element.41), channel_id=1, source_target_pairs={{2,0},{4,2},{6,4},{8,6},{10,8},{12,10},{14,12},{0,14},{3,1},{5,3},... | collective-permute-start | bytes 155528 | tf_op jit(solution)/shard_map/ppermute | solution.py:17
  221.3 25.9 %all_gather.14 = f32[4,3,256]{1,0,2:T(4,128)S(1)} all-gather(f32[4,3,32]{1,0,2:T(4,128)S(1)} %copy.64), channel_id=1, replica_groups=mesh['member'=2,'lon'=8,'lat'=2] {'lon'}, dimensions={2}, use_global_device_ids=true | all-gather | bytes 13824 | tf_op jit(solution)/shard_map/all_gather | solution.py:37
  247.1 0.6 gather_fusion.3
  248.0 7.0 %collective-permute-start.10 = (f32[4,38,3]{2,1,0:T(8,128)S(1)}, f32[4,38,3]{2,1,0:T(8,128)S(1)}, u32[]{:S(2)}, u32[]{:S(2)}) collective-permute-start(f32[4,38,3]{2,1,0:T(8,128)S(1)} %get-tuple-element.28), channel_id=1, source_target_pairs={{0,1},{1,0},{2,3},{3,2},{4,5},{5,4},{6,7},{7,6},{8,9},{9,8},{10,11... | collective-permute-start | bytes 5480 | tf_op jit(solution)/shard_map/ppermute | solution.py:16
  255.2 0.7 collective-permute-done.10
  255.9 0.3 collective-permute-done.11
  256.3 0.4 maximum_maximum_fusion.2
  256.7 36.4 %fusion.54 = f32[4,32,1080]{2,1,0:T(8,128)S(1)} fusion(f32[4,38,1083]{2,1,0:T(8,128)S(1)} %get-tuple-element.27, f32[4,35,1080]{2,1,0:T(8,128)S(1)} %get-tuple-element.39, f32[4,38,1083]{2,1,0:T(8,128)S(1)} %get-tuple-element.26, f32[4,35,1080]{2,1,0:T(8,128)S(1)} %get-tuple-element.38, f32[3,32,1080]{2,1,0:T(8,128)S(1)} %broadcast_multiply_fusion.1, ...), kind=kLoop, calls=%fused_computation.141 | loop fusion | flops 13962240 | bytes 27924676 | tf_op jit(solution)/shard_map/mul | solution.py:93
  293.2 0.7 multiply_reduce_fusion
  293.9 29.6 %psum.37 = f32[]{:T(128)} all-reduce(f32[]{:T(128)} %get-tuple-element.15), channel_id=1, replica_groups=mesh['member'=2,'lon'=8,'lat'=2] {'lon','lat'}, use_global_device_ids=true, to_apply=%region_7.10 | all-reduce | flops 1 | bytes 8 | tf_op jit(solution)/shard_map/psum | solution.py:55
  324.6 4.1 %collective-permute-start.13 = (f32[4,3,1080]{2,1,0:T(4,128)S(1)}, f32[4,3,1080]{2,1,0:T(4,128)S(1)}, u32[]{:S(2)}, u32[]{:S(2)}) collective-permute-start(f32[4,3,1080]{2,1,0:T(4,128)S(1)} %get-tuple-element.37), channel_id=1, source_target_pairs={{2,0},{4,2},{6,4},{8,6},{10,8},{12,10},{14,12},{0,14},{3,1},{5,3},... | collective-permute-start | bytes 155528 | tf_op jit(solution)/shard_map/ppermute | solution.py:17
  328.8 25.2 %all_gather.15 = f32[4,3,256]{1,0,2:T(4,128)S(1)} all-gather(f32[4,3,32]{1,0,2:T(4,128)S(1)} %copy.66), channel_id=1, replica_groups=mesh['member'=2,'lon'=8,'lat'=2] {'lon'}, dimensions={2}, use_global_device_ids=true | all-gather | bytes 13824 | tf_op jit(solution)/shard_map/all_gather | solution.py:37
  354.0 0.6 gather_fusion.4
  354.7 0.6 pad_maximum_fusion.28
  355.5 7.6 %collective-permute-start.14 = (f32[4,38,3]{2,1,0:T(8,128)S(1)}, f32[4,38,3]{2,1,0:T(8,128)S(1)}, u32[]{:S(2)}, u32[]{:S(2)}) collective-permute-start(f32[4,38,3]{2,1,0:T(8,128)S(1)} %get-tuple-element.24), channel_id=1, source_target_pairs={{0,1},{1,0},{2,3},{3,2},{4,5},{5,4},{6,7},{7,6},{8,9},{9,8},{10,11... | collective-permute-start | bytes 5480 | tf_op jit(solution)/shard_map/ppermute | solution.py:16
  363.3 0.7 collective-permute-done.14
  364.1 0.3 collective-permute-done.15
  364.4 0.4 maximum_maximum_fusion.4
  364.8 36.4 %fusion.3 = f32[4,32,1080]{2,1,0:T(8,128)S(1)} fusion(f32[4,38,1083]{2,1,0:T(8,128)S(1)} %get-tuple-element.23, f32[4,35,1080]{2,1,0:T(8,128)S(1)} %get-tuple-element.35, f32[4,38,1083]{2,1,0:T(8,128)S(1)} %get-tuple-element.22, f32[4,35,1080]{2,1,0:T(8,128)S(1)} %get-tuple-element.34, f32[3,32,1080]{2,1,0:T(8,128)S(1)} %broadcast_multiply_fusion, ...), kind=kLoop, calls=%fused_computation.42 | loop fusion | flops 13962240 | bytes 27924676 | tf_op jit(solution)/shard_map/mul | solution.py:93
  401.2 0.7 slice_bitcast_fusion
  401.8 0.8 slice.1702
  (81 shorter events, 3.6 us)
Async XLA Ops:
  0.6 46.1 %copy-start = (s32[256]{0:T(256)S(1)}, s32[256]{0:T(256)}, u32[]{:S(2)}) copy-start(s32[256]{0:T(256)} %param.16) | copy-start | bytes 3076
  0.6 6.3 %copy-start.5 = (f32[3,32,1080]{2,1,0:T(8,128)S(1)}, f32[3,32,1080]{2,1,0:T(8,128)}, u32[]{:S(2)}) copy-start(f32[3,32,1080]{2,1,0:T(8,128)} %param.11) | copy-start | bytes 1244164
  1.7 97.2 %collective-permute-start.4 = (f32[1,3,1080]{2,1,0:T(4,128)S(1)}, f32[1,3,1080]{2,1,0:T(4,128)S(1)}, u32[]{:S(2)}, u32[]{:S(2)}) collective-permute-start(f32[1,3,1080]{2,1,0:T(4,128)S(1)} %get-tuple-element.59), channel_id=1, source_target_pairs={{0,2},{2,4},{4,6},{6,8},{8,10},{10,12},{12,14},{14,0},{1,3},{3,5},... | collective-permute-start | bytes 38888 | tf_op jit(solution)/shard_map/ppermute | solution.py:16
  3.8 3.2 copy-start.1
  3.8 3.2 copy-start.2
  3.8 3.2 copy-start.4
  3.8 95.1 %collective-permute-start.5 = (f32[1,3,1080]{2,1,0:T(4,128)S(1)}, f32[1,3,1080]{2,1,0:T(4,128)S(1)}, u32[]{:S(2)}, u32[]{:S(2)}) collective-permute-start(f32[1,3,1080]{2,1,0:T(4,128)S(1)} %get-tuple-element.60), channel_id=1, source_target_pairs={{2,0},{4,2},{6,4},{8,6},{10,8},{12,10},{14,12},{0,14},{3,1},{5,3},... | collective-permute-start | bytes 38888 | tf_op jit(solution)/shard_map/ppermute | solution.py:17
  7.0 1.0 copy-start.3
  40.8 4.2 %copy-start.6 = (f32[7,7]{1,0:T(8,128)S(1)}, f32[7,7]{1,0:T(8,128)}, u32[]{:S(2)}) copy-start(f32[7,7]{1,0:T(8,128)} %param.17) | copy-start | bytes 592
  40.8 106.1 %collective-permute-start = (f32[4,3,1080]{2,1,0:T(4,128)S(1)}, f32[4,3,1080]{2,1,0:T(4,128)S(1)}, u32[]{:S(2)}, u32[]{:S(2)}) collective-permute-start(f32[4,3,1080]{2,1,0:T(4,128)S(1)} %get-tuple-element.44), channel_id=1, source_target_pairs={{0,2},{2,4},{4,6},{6,8},{8,10},{10,12},{12,14},{14,0},{1,3},{3,5},... | collective-permute-start | bytes 155528 | tf_op jit(solution)/shard_map/ppermute | solution.py:16
  40.9 106.0 %collective-permute-start.1 = (f32[4,3,1080]{2,1,0:T(4,128)S(1)}, f32[4,3,1080]{2,1,0:T(4,128)S(1)}, u32[]{:S(2)}, u32[]{:S(2)}) collective-permute-start(f32[4,3,1080]{2,1,0:T(4,128)S(1)} %get-tuple-element.45), channel_id=1, source_target_pairs={{2,0},{4,2},{6,4},{8,6},{10,8},{12,10},{14,12},{0,14},{3,1},{5,3},... | collective-permute-start | bytes 155528 | tf_op jit(solution)/shard_map/ppermute | solution.py:17
  98.9 15.4 %collective-permute-start.6 = (f32[1,38,3]{2,1,0:T(8,128)S(1)}, f32[1,38,3]{2,1,0:T(8,128)S(1)}, u32[]{:S(2)}, u32[]{:S(2)}) collective-permute-start(f32[1,38,3]{2,1,0:T(8,128)S(1)} %get-tuple-element.53), channel_id=1, source_target_pairs={{0,1},{1,0},{2,3},{3,2},{4,5},{5,4},{6,7},{7,6},{8,9},{9,8},{10,11... | collective-permute-start | bytes 1376 | tf_op jit(solution)/shard_map/ppermute | solution.py:16
  113.6 1.3 collective-permute-start.7
  147.0 1.3 collective-permute-start.2
  147.3 1.3 collective-permute-start.3
  217.0 30.9 %collective-permute-start.8 = (f32[4,3,1080]{2,1,0:T(4,128)S(1)}, f32[4,3,1080]{2,1,0:T(4,128)S(1)}, u32[]{:S(2)}, u32[]{:S(2)}) collective-permute-start(f32[4,3,1080]{2,1,0:T(4,128)S(1)} %get-tuple-element.40), channel_id=1, source_target_pairs={{0,2},{2,4},{4,6},{6,8},{8,10},{10,12},{12,14},{14,0},{1,3},{3,5},... | collective-permute-start | bytes 155528 | tf_op jit(solution)/shard_map/ppermute | solution.py:16
  217.1 30.8 %collective-permute-start.9 = (f32[4,3,1080]{2,1,0:T(4,128)S(1)}, f32[4,3,1080]{2,1,0:T(4,128)S(1)}, u32[]{:S(2)}, u32[]{:S(2)}) collective-permute-start(f32[4,3,1080]{2,1,0:T(4,128)S(1)} %get-tuple-element.41), channel_id=1, source_target_pairs={{2,0},{4,2},{6,4},{8,6},{10,8},{12,10},{14,12},{0,14},{3,1},{5,3},... | collective-permute-start | bytes 155528 | tf_op jit(solution)/shard_map/ppermute | solution.py:17
  248.0 7.9 %collective-permute-start.10 = (f32[4,38,3]{2,1,0:T(8,128)S(1)}, f32[4,38,3]{2,1,0:T(8,128)S(1)}, u32[]{:S(2)}, u32[]{:S(2)}) collective-permute-start(f32[4,38,3]{2,1,0:T(8,128)S(1)} %get-tuple-element.28), channel_id=1, source_target_pairs={{0,1},{1,0},{2,3},{3,2},{4,5},{5,4},{6,7},{7,6},{8,9},{9,8},{10,11... | collective-permute-start | bytes 5480 | tf_op jit(solution)/shard_map/ppermute | solution.py:16
  255.0 1.3 collective-permute-start.11
  324.6 30.8 %collective-permute-start.12 = (f32[4,3,1080]{2,1,0:T(4,128)S(1)}, f32[4,3,1080]{2,1,0:T(4,128)S(1)}, u32[]{:S(2)}, u32[]{:S(2)}) collective-permute-start(f32[4,3,1080]{2,1,0:T(4,128)S(1)} %get-tuple-element.36), channel_id=1, source_target_pairs={{0,2},{2,4},{4,6},{6,8},{8,10},{10,12},{12,14},{14,0},{1,3},{3,5},... | collective-permute-start | bytes 155528 | tf_op jit(solution)/shard_map/ppermute | solution.py:16
  324.6 30.7 %collective-permute-start.13 = (f32[4,3,1080]{2,1,0:T(4,128)S(1)}, f32[4,3,1080]{2,1,0:T(4,128)S(1)}, u32[]{:S(2)}, u32[]{:S(2)}) collective-permute-start(f32[4,3,1080]{2,1,0:T(4,128)S(1)} %get-tuple-element.37), channel_id=1, source_target_pairs={{2,0},{4,2},{6,4},{8,6},{10,8},{12,10},{14,12},{0,14},{3,1},{5,3},... | collective-permute-start | bytes 155528 | tf_op jit(solution)/shard_map/ppermute | solution.py:17
  355.5 8.6 %collective-permute-start.14 = (f32[4,38,3]{2,1,0:T(8,128)S(1)}, f32[4,38,3]{2,1,0:T(8,128)S(1)}, u32[]{:S(2)}, u32[]{:S(2)}) collective-permute-start(f32[4,38,3]{2,1,0:T(8,128)S(1)} %get-tuple-element.24), channel_id=1, source_target_pairs={{0,1},{1,0},{2,3},{3,2},{4,5},{5,4},{6,7},{7,6},{8,9},{9,8},{10,11... | collective-permute-start | bytes 5480 | tf_op jit(solution)/shard_map/ppermute | solution.py:16
  363.1 1.3 collective-permute-start.15
where the time goes:
time: 405 us; the launch traced here: 403 us
  blocking collectives  190 us (47%)
  other arithmetic  148 us (37%)
  starting transfers between devices  47.8 us (12%)
  local copies, waits for them, and re-layouts  8.28 us (2%)
  waiting for transfers between devices  4.17 us (1%)
    mul x3, other arithmetic, shards(): fresh = ocean[None] * (0.5 * fields + 0.5 * averaged)  109 us
    all_gather x4, blocking collectives, extend(): whole_top = lax.all_gather(top, 'lon', axis=2, tiled=True)  100 us
    psum x3, blocking collectives, ocean_excess(): excess, ocean_total = lax.psum((local_excess, count), ('lon', 'lat'))  89.8 us
    div x1, other arithmetic, shards(): smooth(extend(fields, fold_partner, width), kernel_weights, ncols, nrows)  31.9 us
    ppermute x8, starting transfers between devices, padded_2(): before = lax.ppermute(last, axis, up)  31.6 us
    ppermute x8, starting transfers between devices, padded_2(): after = lax.ppermute(first, axis, down)  16.2 us
  transfers between devices with their start and end apart: 16, of which 8 were waited for; matrix products, arithmetic and copies ran while one was open for 10% of the time, Pallas kernels for 0%

commit v1 on v0

v1 whole, which is shorter than its diff:
```python
import functools

import jax
import jax.numpy as jnp
from jax import lax
from jax.experimental import pallas as pl
from jax.experimental.pallas import tpu as pltpu
from jax.sharding import PartitionSpec as P

ITERS = 3
LANES = 128
SUB = 8
MESH = pl.DeviceIdType.MESH
F32 = jnp.float32


def kernel(
    nlon, nlat, nrows, R, L, side,
    w_ref, partner_ref, e_ref, s_ref, conc_ref, class_ref, mask_ref,
    stress_ref, damage_ref, mean_ref,
    Z, Y, X, T, load, base, ocean, rlim, rden, state, C, G, XC, D,
    up_out, down_out, low_in, high_in, ocean_out, ocean_in,
    slab, lat_in, fold_in, stat, stat_in, stage, tops,
    row_send, row_recv, oc_send, oc_recv, lat_send, lat_recv, fold_send, fold_recv, stat_send, stat_recv,
):
    width = side // 2
    n = nlon * nlat
    ncols = R * SUB
    lon, lat = lax.axis_index("lon"), lax.axis_index("lat")
    member = lax.axis_index("member")
    is_last = lat == nlat - 1
    me = lon * nlat + lat
    nb = nrows - (L - LANES)

    def dev(a, b):
        return (member, a, b)

    def peer(d):
        other = lax.rem(me + d, n)
        return dev(other // nlat, lax.rem(other, nlat))

    right, left = lax.rem(lon + 1, nlon), lax.rem(lon + nlon - 1, nlon)
    other_lat = lax.rem(lat + 1, nlat)

    barrier = pltpu.get_barrier_semaphore()

    def greet(d, c):
        pl.semaphore_signal(barrier, inc=1, device_id=peer(d), device_id_type=MESH)
        return c

    lax.fori_loop(1, n, greet, 0)

    sub = lax.broadcasted_iota(jnp.int32, (SUB, L), 0)
    lane = lax.broadcasted_iota(jnp.int32, (SUB, LANES), 1)

    for ref in (load, base, ocean, rlim, state, stage):
        ref[...] = jnp.zeros(ref.shape, F32)
    tiles = L // LANES
    span = [min(LANES, nrows - t * LANES) for t in range(tiles)]
    sources = (
        mask_ref, conc_ref, class_ref, s_ref.at[0], s_ref.at[1], s_ref.at[2], e_ref.at[0], e_ref.at[1], e_ref.at[2]
    )
    for t in range(tiles):
        cut = slice(t * LANES, t * LANES + span[t])
        for k, source in enumerate(sources):
            stage[k, t, :, : span[t]] = source[:, cut].astype(F32)
        for r in range(R):
            oc, conc, grade, s1, s2, s3, one, two, shear = (
                stage[k, t, pl.ds(r, SUB, stride=R), :][:, : span[t]] for k in range(9)
            )
            ocean[r, :, cut] = oc
            base[r, :, cut] = conc * jnp.exp(-2.0 * (1.0 - conc))
            rlim[r, :, cut] = 1.0 / (0.6 * conc)
            state[0, r, :, cut] = oc * 0.1 * grade * conc
            for k, part in enumerate((s1, s2, s3)):
                state[1 + k, r, :, cut] = oc * part
            load[0, r, :, cut] = (one + two / 3.0) / (8.0 / 9.0)
            load[1, r, :, cut] = (two + one / 3.0) / (8.0 / 9.0)
            load[2, r, :, cut] = (shear / (4.0 / 3.0)) / (8.0 / 9.0)
    count = jnp.zeros((1, L), F32)
    for r in range(R):
        Z[8, r] = ocean[r]
        count = count + jnp.sum(ocean[r], axis=0, keepdims=True)
    count = functools.reduce(
        lambda a, b: a + b, [count[:, t * LANES : (t + 1) * LANES] for t in range(L // LANES)]
    )
    ocean_out[...] = jnp.zeros(ocean_out.shape, F32)
    for m in range(width):
        ocean_out[0, m : m + 1, :] = ocean[R - width + m, SUB - 1 : SUB, :]
        ocean_out[1, m : m + 1, :] = ocean[m, 0:1, :]
    slab[...] = jnp.zeros(slab.shape, F32)
    up_out[...] = jnp.zeros(up_out.shape, F32)
    down_out[...] = jnp.zeros(down_out.shape, F32)

    pl.semaphore_wait(barrier, n - 1)

    def ocean_copy(k, to):
        return pltpu.make_async_remote_copy(
            src_ref=ocean_out.at[k], dst_ref=ocean_in.at[k], send_sem=oc_send.at[k],
            recv_sem=oc_recv.at[k], device_id=dev(to, lat), device_id_type=MESH,
        )

    ocean_copy(0, right).start()
    ocean_copy(1, left).start()

    def conv(f, c):
        for r in range(R):
            X[width + r] = Z[f, r]
        for m in range(width):
            X[m] = jnp.where(sub == 0, 0.0, pltpu.roll(Z[f, m + R - width], 1, 0))
            X[R + width + m] = jnp.where(sub == SUB - 1, 0.0, pltpu.roll(Z[f, m], SUB - 1, 0))
        for b in range(side):
            acc = [None] * R
            for p in range(R + 2 * width):
                x = X[p]
                for r in range(R):
                    a = p - r
                    if 0 <= a < side:
                        term = w_ref[a, b] * x
                        acc[r] = term if acc[r] is None else acc[r] + term
            for r in range(R):
                moved = acc[r] if b == width else pltpu.roll(acc[r], (width - b) % L, 1)
                if b == 0:
                    Y[f, r] = moved
                else:
                    Y[f, r] = Y[f, r] + moved
        return c

    def row_correction(halos):
        for r in range(width):
            total = None
            for b in range(side):
                t = None
                for m in range(r, width):
                    d = m - r
                    w = jnp.where(sub < 4, w_ref[d, b], w_ref[side - 1 - d, b])
                    term = w * halos[m]
                    t = term if t is None else t + term
                t = t if b == width else pltpu.roll(t, (width - b) % L, 1)
                total = t if total is None else total + t
            C[r] = total

    def add_rows(f, c):
        for r in range(width):
            Y[f, r] = Y[f, r] + jnp.where(sub == 0, C[r, c : c + 1, :], 0.0)
            Y[f, R - 1 - r] = Y[f, R - 1 - r] + jnp.where(sub == SUB - 1, C[r, 4 + c : 5 + c, :], 0.0)

    def add_columns(f):
        for r in range(R):
            total = None
            for b in range(side):
                t = None
                for a in range(side):
                    term = w_ref[a, b] * XC[r + a]
                    t = term if t is None else t + term
                t = t if b == width else pltpu.roll(t, (width - b) % LANES, 1)
                total = t if total is None else total + t
            Y[f, r, :, L - LANES :] = Y[f, r, :, L - LANES :] + jnp.where(
                (lane >= nb - width) & (lane < nb), total, 0.0
            )
            Y[f, r, :, :LANES] = Y[f, r, :, :LANES] + jnp.where(lane < width, total, 0.0)

    def ghost(at, factor_of):
        for p in range(R + 2 * width):
            north = jnp.where(
                is_last,
                pltpu.roll(factor_of(1, p), (nb - 16 - at) % LANES, 1),
                pltpu.roll(factor_of(0, p), (nb - at) % LANES, 1),
            )
            south = jnp.where(
                lat > 0, pltpu.roll(factor_of(0, p), (LANES - width - 64 - at) % LANES, 1), 0.0
            )
            XC[p] = jnp.where(
                (lane >= nb) & (lane < nb + width), north,
                jnp.where(lane >= LANES - width, south, 0.0),
            )

    def iteration(it, carry):
        excess = jnp.zeros((SUB, L), F32)
        for r in range(R):
            oc = ocean[r]
            damage = state[0, r]
            keep = 1.0 - damage
            theta = 0.5 / (keep * keep)
            scale = oc / (1.0 + theta)
            bk = base[r] * keep
            el = [scale * (state[1 + k, r] + bk * load[k, r]) for k in range(3)]
            half = (el[0] - el[1]) * 0.5
            tau = jnp.sqrt(half * half + el[2] * el[2] + 0.25)
            over = jnp.maximum((tau + 0.35 * (el[0] + el[1])) * rlim[r], 1.0)
            q = oc * (1.0 - 1.0 / over)
            excess = excess + oc * (over - 1.0)
            Z[0, r] = damage
            Z[4, r] = keep * q
            for k in range(3):
                Z[1 + k, r] = el[k]
                Z[5 + k, r] = -(el[k] * q)
            T[r] = q
        for m in range(width):
            hi = R - width + m
            q_row = 4 + m
            for f in range(4):
                at = 4 * m + f
                up_out[it, at // 8, at % 8 : at % 8 + 1, :] = Z[f, hi, SUB - 1 : SUB, :]
                down_out[it, at // 8, at % 8 : at % 8 + 1, :] = Z[f, m, 0:1, :]
            up_out[it, 1, q_row : q_row + 1, :] = T[hi, SUB - 1 : SUB, :]
            down_out[it, 1, q_row : q_row + 1, :] = T[m, 0:1, :]
        up = pltpu.make_async_remote_copy(
            src_ref=up_out.at[it], dst_ref=low_in.at[it], send_sem=row_send.at[it, 0],
            recv_sem=row_recv.at[it, 0], device_id=dev(right, lat), device_id_type=MESH,
        )
        down = pltpu.make_async_remote_copy(
            src_ref=down_out.at[it], dst_ref=high_in.at[it], send_sem=row_send.at[it, 1],
            recv_sem=row_recv.at[it, 1], device_id=dev(left, lat), device_id_type=MESH,
        )
        lines = jnp.sum(excess, axis=0, keepdims=True)
        stat[it, 0:1, :] = functools.reduce(
            lambda a, b: a + b, [lines[:, t * LANES : (t + 1) * LANES] for t in range(L // LANES)]
        )
        stat[it, 1:2, :] = count

        def stat_copy(d):
            return pltpu.make_async_remote_copy(
                src_ref=stat.at[it], dst_ref=stat_in.at[it, d], send_sem=stat_send.at[it, d],
                recv_sem=stat_recv.at[it, d], device_id=peer(d), device_id_type=MESH,
            )

        def start_stat(d, c):
            stat_copy(d).start()
            return c

        lax.fori_loop(1, n, start_stat, 0)
        up.start()
        down.start()

        for r in range(R):
            value = jnp.zeros((SUB, LANES), F32)
            for f in range(9):
                at = 3 * f if f < 4 else (32 + 3 * (f - 4) if f < 8 else 12)
                first = Z[f, r, :, :LANES]
                last = Z[f, r, :, L - LANES :]
                value = jnp.where(
                    (lane >= at) & (lane < at + width), pltpu.roll(first, at, 1), value
                )
                value = jnp.where(
                    (lane >= at + 64) & (lane < at + 64 + width),
                    pltpu.roll(last, (at + 64 + width - nb) % LANES, 1), value,
                )
                for k in range(width):
                    value = jnp.where(
                        lane == at + 16 + k, pltpu.roll(last, (at + 16 + k - (nb - 1 - k)) % LANES, 1), value
                    )
            slab[it, r * SUB : (r + 1) * SUB, :] = value

        def lat_copy(k):
            to = lax.rem(lon + 1 - k + nlon, nlon)
            return pltpu.make_async_remote_copy(
                src_ref=slab.at[it], dst_ref=lat_in.at[it, k], send_sem=lat_send.at[it, k],
                recv_sem=lat_recv.at[it, k], device_id=dev(to, other_lat), device_id_type=MESH,
            )

        def fold_copy(d):
            return pltpu.make_async_remote_copy(
                src_ref=slab.at[it], dst_ref=fold_in.at[it, pl.ds(pl.multiple_of(lon * ncols, SUB), ncols), :],
                send_sem=fold_send.at[it, d], recv_sem=fold_recv.at[it, d],
                device_id=dev(lax.rem(lon + d, nlon), lat), device_id_type=MESH,
            )

        for k in range(3):
            lat_copy(k).start()

        @pl.when(is_last)
        def _():
            def start_fold(d, c):
                fold_copy(d).start()
                return c

            lax.fori_loop(1, nlon, start_fold, 0)
            fold_in[it, pl.ds(pl.multiple_of(lon * ncols, SUB), ncols), :] = slab[it]

        lax.fori_loop(0, jnp.where(it == 0, 9, 8), conv, 0)

        def wait_stat(d, c):
            stat_copy(d).wait()
            return c

        lax.fori_loop(1, n, wait_stat, 0)
        stat_in[it, 0] = stat[it]

        def add_stat(d, total):
            return total + stat_in[it, d]

        total = lax.fori_loop(1, n, add_stat, stat_in[it, 0])
        sums = jnp.sum(total, axis=1, keepdims=True)
        mean = sums[0:1] / (sums[1:2] + 1.0)
        factor = 1.0 / (1.0 + 2.0 * mean)
        mean_ref[pl.ds(it, 1), :] = jnp.broadcast_to(mean, (1, LANES))

        up.wait()
        down.wait()
        for k in range(3):
            lat_copy(k).wait()

        @pl.when(is_last)
        def _():
            def wait_fold(d, c):
                fold_copy(d).wait()
                return c

            lax.fori_loop(1, nlon, wait_fold, 0)

            tops[...] = fold_in[it]

            def pick(i, c):
                where = lax.rem(lon * ncols + i - width + nlon * ncols, nlon * ncols)
                p = partner_ref[where]
                col = lax.rem(p, ncols)
                row = (p // ncols) * ncols + lax.rem(col, R) * SUB + col // R
                D[pl.ds(i, 1), :] = tops[pl.ds(row, 1), :]
                return c

            lax.fori_loop(0, ncols + 2 * width, pick, 0)
            for p in range(R + 2 * width):
                G[1, p] = D[pl.ds(p, SUB, stride=R), :]

        @pl.when(jnp.logical_not(is_last))
        def _():
            for p in range(R + 2 * width):
                G[1, p] = jnp.zeros((SUB, LANES), F32)

        small = lax.broadcasted_iota(jnp.int32, (SUB, LANES), 0)
        for r in range(R):
            G[0, width + r] = lat_in[it, 1, r * SUB : (r + 1) * SUB, :]
        for m in range(width):
            r = m + R - width
            at = slice(r * SUB, (r + 1) * SUB)
            G[0, m] = jnp.where(
                small == 0, pltpu.roll(lat_in[it, 0, at, :], 1, 0), pltpu.roll(lat_in[it, 1, at, :], 1, 0)
            )
            at = slice(m * SUB, (m + 1) * SUB)
            G[0, R + width + m] = jnp.where(
                small == SUB - 1,
                pltpu.roll(lat_in[it, 2, at, :], SUB - 1, 0), pltpu.roll(lat_in[it, 1, at, :], SUB - 1, 0),
            )

        @pl.when(it == 0)
        def _():
            ocean_copy(0, right).wait()
            ocean_copy(1, left).wait()
            row_correction([
                jnp.concatenate([
                    jnp.broadcast_to(ocean_in[0, m : m + 1, :], (4, L)),
                    jnp.broadcast_to(ocean_in[1, width - 1 - m : width - m, :], (4, L)),
                ], axis=0)
                for m in range(width)
            ])
            add_rows(8, 0)
            ghost(12, lambda k, p: G[k, p])
            add_columns(8)
            for r in range(R):
                rden[r] = 1.0 / (Y[8, r] + 1.0)

        head = lax.broadcasted_iota(jnp.int32, (4, L), 0) == 0

        def local_rows(ref, m):
            fq = factor * ref[it, 1, 4 + m : 5 + m, :]
            at = 4 * m
            field = ref[it, at // 8, at % 8 : at % 8 + 4, :]
            return field * (1.0 - fq) + jnp.where(head, fq, 0.0)

        row_correction([
            jnp.concatenate([local_rows(low_in, m), local_rows(high_in, width - 1 - m)], axis=0)
            for m in range(width)
        ])
        for k in range(2):
            for p in range(R + 2 * width):
                g = G[k, p]
                G[k, p] = g + factor * pltpu.roll(g, LANES - 32, 1)
        for f in range(4):
            for r in range(R):
                Y[f, r] = Y[f, r] + factor * Y[4 + f, r]
            add_rows(f, f)
            ghost(3 * f, lambda k, p: G[k, p])
            add_columns(f)
            for r in range(R):
                state[f, r] = (0.5 * ocean[r]) * (Z[f, r] + factor * Z[4 + f, r] + Y[f, r] * rden[r])
        return carry

    lax.fori_loop(0, ITERS, iteration, 0)
    outputs = (damage_ref, stress_ref.at[0], stress_ref.at[1], stress_ref.at[2])
    for t in range(tiles):
        cut = slice(t * LANES, t * LANES + span[t])
        for k, target in enumerate(outputs):
            for r in range(R):
                stage[k, t, pl.ds(r, SUB, stride=R), :] = state[k, r, :, t * LANES : (t + 1) * LANES]
            target[:, cut] = stage[k, t, :, : span[t]]


def shards(nlon, nlat, strain_rate, stress_start, concentration, cell_class, land_mask, fold_partner, kernel_weights):
    ncols, nrows = concentration.shape
    side = kernel_weights.shape[0]
    width = side // 2
    R = ncols // SUB
    L = -(-(nrows + 2 * width) // LANES) * LANES
    n = nlon * nlat
    V = lambda *shape: pltpu.VMEM(shape, F32)
    S = lambda *shape: pltpu.SemaphoreType.DMA(shape)
    planes = R + 2 * width
    stress, damage, mean = pl.pallas_call(
        functools.partial(kernel, nlon, nlat, nrows, R, L, side),
        out_shape=(
            jax.ShapeDtypeStruct((3, ncols, nrows), F32),
            jax.ShapeDtypeStruct((ncols, nrows), F32),
            jax.ShapeDtypeStruct((ITERS, LANES), F32),
        ),
        in_specs=[pl.BlockSpec(memory_space=pltpu.SMEM)] * 2 + [pl.BlockSpec(memory_space=pltpu.VMEM)] * 5,
        out_specs=(pl.BlockSpec(memory_space=pltpu.VMEM),) * 3,
        scratch_shapes=[
            V(9, R, SUB, L), V(9, R, SUB, L), V(planes, SUB, L), V(R, SUB, L),
            V(3, R, SUB, L), V(R, SUB, L), V(R, SUB, L), V(R, SUB, L), V(R, SUB, L), V(4, R, SUB, L),
            V(width, SUB, L), V(2, planes, SUB, LANES), V(planes, SUB, LANES),
            V(-(-(ncols + 2 * width) // SUB) * SUB, LANES),
            V(ITERS, 2, SUB, L), V(ITERS, 2, SUB, L), V(ITERS, 2, SUB, L), V(ITERS, 2, SUB, L),
            V(2, SUB, L), V(2, SUB, L),
            V(ITERS, ncols, LANES), V(ITERS, 3, ncols, LANES), V(ITERS, nlon * ncols, LANES),
            V(ITERS, 2, LANES), V(ITERS, n, 2, LANES), V(9, L // LANES, ncols, LANES), V(nlon * ncols, LANES),
            S(ITERS, 2), S(ITERS, 2), S(2), S(2), S(ITERS, 3), S(ITERS, 3), S(ITERS, nlon), S(ITERS, nlon),
            S(ITERS, n), S(ITERS, n),
        ],
        compiler_params=pltpu.CompilerParams(
            collective_id=0, has_side_effects=True, vmem_limit_bytes=48 * 1024 * 1024
        ),
    )(kernel_weights, fold_partner, strain_rate, stress_start, concentration, cell_class, land_mask)
    return stress, damage, mean[:, 0]


def solution(mesh):
    in_specs = (
        P(None, "lon", "lat"),
        P(None, "lon", "lat"),
        P("lon", "lat"),
        P(("member", "lon"), "lat"),
        P("lon", "lat"),
        P(),
        P(),
    )
    out_specs = (P(None, ("member", "lon"), "lat"), P(("member", "lon"), "lat"), P("member"))
    body = functools.partial(shards, mesh.shape["lon"], mesh.shape["lat"])
    return jax.shard_map(body, mesh=mesh, in_specs=in_specs, out_specs=out_specs, check_vma=False)
```

time: 405 us -> 44.3 us (0.11)
  blocking collectives: 190 us -> 0 us
  other arithmetic: 148 us -> 0 us
  starting transfers between devices: 47.8 us -> 0 us
  Pallas kernels: 0 us -> 35.2 us
  waiting for transfers between devices: 4.17 us -> 0 us
    mul x9 -> x0, other arithmetic: 110 us -> none  [the longest x3 109 us: shards(): fresh = ocean[None] * (0.5 * fields + 0.5 * averaged)]
    all_gather x4 -> x0, blocking collectives: 100 us -> none  [extend(): whole_top = lax.all_gather(top, 'lon', axis=2, tiled=True)]
    psum x3 -> x0, blocking collectives: 89.8 us -> none  [ocean_excess(): excess, ocean_total = lax.psum((local_excess, count), ('lon', 'lat'))]
    ppermute x16 -> x0, starting transfers between devices: 47.8 us -> none  [the longest x8 31.6 us: padded_2(): before = lax.ppermute(last, axis, up)]
    pallas_call x0 -> x1, Pallas kernels: none -> 35.2 us  [shards(): pl.pallas_call(functools.partial(kernel, nlon, nlat, nrows, R, L, side),...]
    div x6 -> x0, other arithmetic: 32.2 us -> none  [the longest x1 31.9 us: shards(): smooth(extend(fields, fold_partner, width), kernel_weights, ncols, nrows)]
    unnamed x14 -> x16, local copies, waits for them, and re-layouts: 0.94 us -> 7.53 us
    ppermute x16 -> x0, waiting for transfers between devices: 4.17 us -> none  [the longest x8 2.76 us: padded_2(): before = lax.ppermute(last, axis, up)]
  transfers between devices with their start and end apart: 16 -> 0, of which waited for: 8 -> 0; matrix products, arithmetic and copies ran while one was open for 10% -> 0% of each run, Pallas kernels for 0% -> 0%
where the time goes in v1:
time: 44.3 us; the launch traced here: 44 us
  Pallas kernels  35.2 us (79%)
  local copies, waits for them, and re-layouts  8.16 us (18%)
  between operations  0.66 us (1%)
    pallas_call x1, Pallas kernels, shards(): pl.pallas_call(functools.partial(kernel, nlon, nlat, nrows, R, L, side),...  35.2 us
    unnamed x16, local copies, waits for them, and re-layouts  7.53 us

profile of v1, /device:TPU:1, one launch (start us, length us, event | category | flops | bytes accessed | tf_op | source)
XLA Modules:
  0.0 44.0 jit_solution(16504847366999478214)
XLA Ops:
  0.6 0.0 copy-start
  0.6 1.0 %copy-done = f32[3,32,1080]{2,1,0:T(8,128)S(1)} copy-done((f32[3,32,1080]{2,1,0:T(8,128)S(1)}, f32[3,32,1080]{2,1,0:T(8,128)}, u32[]{:S(2)}) %copy-start) | copy-done | bytes 414744
  1.6 0.0 copy-start.1
  1.6 1.0 %copy-done.1 = f32[3,32,1080]{2,1,0:T(8,128)S(1)} copy-done((f32[3,32,1080]{2,1,0:T(8,128)S(1)}, f32[3,32,1080]{2,1,0:T(8,128)}, u32[]{:S(2)}) %copy-start.1) | copy-done | bytes 414744
  2.7 0.0 copy-start.2
  2.7 0.9 %copy-done.2 = f32[32,1080]{1,0:T(8,128)S(1)} copy-done((f32[32,1080]{1,0:T(8,128)S(1)}, f32[32,1080]{1,0:T(8,128)}, u32[]{:S(2)}) %copy-start.2) | copy-done | bytes 138264
  3.6 0.0 copy-start.3
  3.6 0.9 %copy-done.3 = s32[32,1080]{1,0:T(8,128)S(1)} copy-done((s32[32,1080]{1,0:T(8,128)S(1)}, s32[32,1080]{1,0:T(8,128)}, u32[]{:S(2)}) %copy-start.3) | copy-done | bytes 138264
  4.5 0.0 copy-start.4
  4.5 0.9 %copy-done.4 = s32[32,1080]{1,0:T(8,128)S(1)} copy-done((s32[32,1080]{1,0:T(8,128)S(1)}, s32[32,1080]{1,0:T(8,128)}, u32[]{:S(2)}) %copy-start.4) | copy-done | bytes 138264
  5.4 0.0 copy-start.5
  5.4 0.7 %copy-done.5 = f32[7,7]{1,0:T(8,128)S(1)} copy-done((f32[7,7]{1,0:T(8,128)S(1)}, f32[7,7]{1,0:T(8,128)}, u32[]{:S(2)}) %copy-start.5) | copy-done | bytes 220
  6.1 0.0 copy-start.6
  6.1 0.7 %copy-done.6 = s32[256]{0:T(256)S(1)} copy-done((s32[256]{0:T(256)S(1)}, s32[256]{0:T(256)}, u32[]{:S(2)}) %copy-start.6) | copy-done | bytes 1048
  6.8 35.2 %shard_map.94 = (f32[3,32,1080]{2,1,0:T(8,128)S(1)}, f32[32,1080]{1,0:T(8,128)S(1)}, f32[3,128]{1,0:T(4,128)S(1)}) custom-call(f32[7,7]{1,0:T(8,128)S(1)} %copy-done.5, s32[256]{0:T(256)S(1)} %copy-done.6, f32[3,32,1080]{2,1,0:T(8,128)S(1)} %copy-done, f32[3,32,1080]{2,1,0:T(8,128)S(1)} %copy-done.1, f32[32,1080]{1,0:T(8,128)S(1)} %copy-done.2, ...), custom_call_target="tpu_custom_call" | custom-call | tf_op jit(solution)/shard_map/pallas_call | solution.py:409
  42.0 0.6 %slice_reduce_fusion = f32[3]{0:T(128)} fusion(f32[3,128]{1,0:T(4,128)S(1)} %get-tuple-element.8), kind=kLoop, calls=%fused_computation | loop fusion | bytes 24 | tf_op jit(solution)/shard_map/slice | solution.py:434
  42.6 0.8 %copy.12 = f32[3,32,1080]{2,1,0:T(8,128)} copy(f32[3,32,1080]{2,1,0:T(8,128)S(1)} %get-tuple-element.12) | data formatting | bytes 829440
  43.4 0.7 %copy.13 = f32[32,1080]{1,0:T(8,128)} copy(f32[32,1080]{1,0:T(8,128)S(1)} %get-tuple-element.13) | data formatting | bytes 276480
Async XLA Ops:
  0.6 1.0 %copy-start = (f32[3,32,1080]{2,1,0:T(8,128)S(1)}, f32[3,32,1080]{2,1,0:T(8,128)}, u32[]{:S(2)}) copy-start(f32[3,32,1080]{2,1,0:T(8,128)} %e_ref.1) | copy-start | bytes 1244164
  1.6 1.0 %copy-start.1 = (f32[3,32,1080]{2,1,0:T(8,128)S(1)}, f32[3,32,1080]{2,1,0:T(8,128)}, u32[]{:S(2)}) copy-start(f32[3,32,1080]{2,1,0:T(8,128)} %s_ref.1) | copy-start | bytes 1244164
  2.7 0.9 %copy-start.2 = (f32[32,1080]{1,0:T(8,128)S(1)}, f32[32,1080]{1,0:T(8,128)}, u32[]{:S(2)}) copy-start(f32[32,1080]{1,0:T(8,128)} %conc_ref.1) | copy-start | bytes 414724
  3.6 0.9 %copy-start.3 = (s32[32,1080]{1,0:T(8,128)S(1)}, s32[32,1080]{1,0:T(8,128)}, u32[]{:S(2)}) copy-start(s32[32,1080]{1,0:T(8,128)} %class_ref.1) | copy-start | bytes 414724
  4.5 0.9 %copy-start.4 = (s32[32,1080]{1,0:T(8,128)S(1)}, s32[32,1080]{1,0:T(8,128)}, u32[]{:S(2)}) copy-start(s32[32,1080]{1,0:T(8,128)} %mask_ref.1) | copy-start | bytes 414724
  5.4 0.7 %copy-start.5 = (f32[7,7]{1,0:T(8,128)S(1)}, f32[7,7]{1,0:T(8,128)}, u32[]{:S(2)}) copy-start(f32[7,7]{1,0:T(8,128)} %w_ref.1) | copy-start | bytes 592
  6.1 0.7 %copy-start.6 = (s32[256]{0:T(256)S(1)}, s32[256]{0:T(256)}, u32[]{:S(2)}) copy-start(s32[256]{0:T(256)} %partner_ref.1) | copy-start | bytes 3076

commit v2 on v1

--- a/solution.py
+++ b/solution.py
@@ -16,11 +16,12 @@
 
 def kernel(
     nlon, nlat, nrows, R, L, side,
-    w_ref, partner_ref, e_ref, s_ref, conc_ref, class_ref, mask_ref,
+    w_ref, partner_ref, e_hbm, s_hbm, conc_hbm, class_hbm, mask_hbm,
     stress_ref, damage_ref, mean_ref,
-    Z, Y, X, T, load, base, ocean, rlim, rden, state, C, G, XC, D,
+    Z, Y, X, load, base, ocean, rlim, rden, state, C, G, XC, D,
     up_out, down_out, low_in, high_in, ocean_out, ocean_in,
-    slab, lat_in, fold_in, stat, stat_in, stage, tops,
+    slab, lat_in, fold_in, stat, stat_in, stage, tops, HQ, HL,
+    e_ref, s_ref, conc_ref, class_ref, mask_ref, in_sem,
     row_send, row_recv, oc_send, oc_recv, lat_send, lat_recv, fold_send, fold_recv, stat_send, stat_recv,
 ):
     width = side // 2
@@ -42,6 +43,14 @@
     right, left = lax.rem(lon + 1, nlon), lax.rem(lon + nlon - 1, nlon)
     other_lat = lax.rem(lat + 1, nlat)
 
+    loads = [
+        pltpu.make_async_copy(a, b, in_sem.at[k])
+        for k, (a, b) in enumerate((
+            (mask_hbm, mask_ref), (conc_hbm, conc_ref), (class_hbm, class_ref), (s_hbm, s_ref), (e_hbm, e_ref)
+        ))
+    ]
+    for copy in loads:
+        copy.start()
     barrier = pltpu.get_barrier_semaphore()
 
     def greet(d, c):
@@ -55,6 +64,12 @@
 
     for ref in (load, base, ocean, rlim, state, stage):
         ref[...] = jnp.zeros(ref.shape, F32)
+    slab[...] = jnp.zeros(slab.shape, F32)
+    ocean_out[...] = jnp.zeros(ocean_out.shape, F32)
+    HQ[...] = jnp.zeros(HQ.shape, F32)
+    HL[...] = jnp.zeros(HL.shape, F32)
+    for copy in loads:
+        copy.wait()
     tiles = L // LANES
     span = [min(LANES, nrows - t * LANES) for t in range(tiles)]
     sources = (
@@ -84,13 +99,11 @@
     count = functools.reduce(
         lambda a, b: a + b, [count[:, t * LANES : (t + 1) * LANES] for t in range(L // LANES)]
     )
-    ocean_out[...] = jnp.zeros(ocean_out.shape, F32)
     for m in range(width):
+        ocean_out[0, 4 + m : 5 + m, :] = rlim[R - width + m, SUB - 1 : SUB, :]
+        ocean_out[1, 4 + m : 5 + m, :] = rlim[m, 0:1, :]
         ocean_out[0, m : m + 1, :] = ocean[R - width + m, SUB - 1 : SUB, :]
         ocean_out[1, m : m + 1, :] = ocean[m, 0:1, :]
-    slab[...] = jnp.zeros(slab.shape, F32)
-    up_out[...] = jnp.zeros(up_out.shape, F32)
-    down_out[...] = jnp.zeros(down_out.shape, F32)
 
     pl.semaphore_wait(barrier, n - 1)
 
@@ -160,16 +173,10 @@
             )
             Y[f, r, :, :LANES] = Y[f, r, :, :LANES] + jnp.where(lane < width, total, 0.0)
 
-    def ghost(at, factor_of):
+    def ghost(at):
         for p in range(R + 2 * width):
-            north = jnp.where(
-                is_last,
-                pltpu.roll(factor_of(1, p), (nb - 16 - at) % LANES, 1),
-                pltpu.roll(factor_of(0, p), (nb - at) % LANES, 1),
-            )
-            south = jnp.where(
-                lat > 0, pltpu.roll(factor_of(0, p), (LANES - width - 64 - at) % LANES, 1), 0.0
-            )
+            north = pltpu.roll(G[1, p], (nb - at) % LANES, 1)
+            south = jnp.where(lat > 0, pltpu.roll(G[0, p], (LANES - width - at) % LANES, 1), 0.0)
             XC[p] = jnp.where(
                 (lane >= nb) & (lane < nb + width), north,
                 jnp.where(lane >= LANES - width, south, 0.0),
@@ -195,16 +202,11 @@
             for k in range(3):
                 Z[1 + k, r] = el[k]
                 Z[5 + k, r] = -(el[k] * q)
-            T[r] = q
         for m in range(width):
             hi = R - width + m
-            q_row = 4 + m
             for f in range(4):
-                at = 4 * m + f
-                up_out[it, at // 8, at % 8 : at % 8 + 1, :] = Z[f, hi, SUB - 1 : SUB, :]
-                down_out[it, at // 8, at % 8 : at % 8 + 1, :] = Z[f, m, 0:1, :]
-            up_out[it, 1, q_row : q_row + 1, :] = T[hi, SUB - 1 : SUB, :]
-            down_out[it, 1, q_row : q_row + 1, :] = T[m, 0:1, :]
+                up_out[it, m, f : f + 1, :] = Z[f, hi, SUB - 1 : SUB, :]
+                down_out[it, m, f : f + 1, :] = Z[f, m, 0:1, :]
         up = pltpu.make_async_remote_copy(
             src_ref=up_out.at[it], dst_ref=low_in.at[it], send_sem=row_send.at[it, 0],
             recv_sem=row_recv.at[it, 0], device_id=dev(right, lat), device_id_type=MESH,
@@ -233,35 +235,32 @@
         up.start()
         down.start()
 
-        for r in range(R):
-            value = jnp.zeros((SUB, LANES), F32)
+        edge = jnp.zeros((SUB, LANES), F32)
+        top = jnp.zeros((SUB, LANES), F32)
+        for r in range(R):
             for f in range(9):
-                at = 3 * f if f < 4 else (32 + 3 * (f - 4) if f < 8 else 12)
+                at = 32 * r + (3 * f if f < 4 else (16 + 3 * (f - 4) if f < 8 else 12))
                 first = Z[f, r, :, :LANES]
                 last = Z[f, r, :, L - LANES :]
-                value = jnp.where(
-                    (lane >= at) & (lane < at + width), pltpu.roll(first, at, 1), value
+                both = jnp.where(
+                    is_last, pltpu.roll(first, at, 1), pltpu.roll(last, (at + width - nb) % LANES, 1)
                 )
-                value = jnp.where(
-                    (lane >= at + 64) & (lane < at + 64 + width),
-                    pltpu.roll(last, (at + 64 + width - nb) % LANES, 1), value,
-                )
+                edge = jnp.where((lane >= at) & (lane < at + width), both, edge)
                 for k in range(width):
-                    value = jnp.where(
-                        lane == at + 16 + k, pltpu.roll(last, (at + 16 + k - (nb - 1 - k)) % LANES, 1), value
-                    )
-            slab[it, r * SUB : (r + 1) * SUB, :] = value
+                    top = jnp.where(lane == at + k, pltpu.roll(last, (at + k - (nb - 1 - k)) % LANES, 1), top)
+        slab[it, 0] = edge
+        slab[it, 1] = top
 
         def lat_copy(k):
             to = lax.rem(lon + 1 - k + nlon, nlon)
             return pltpu.make_async_remote_copy(
-                src_ref=slab.at[it], dst_ref=lat_in.at[it, k], send_sem=lat_send.at[it, k],
+                src_ref=slab.at[it, 0], dst_ref=lat_in.at[it, k], send_sem=lat_send.at[it, k],
                 recv_sem=lat_recv.at[it, k], device_id=dev(to, other_lat), device_id_type=MESH,
             )
 
         def fold_copy(d):
             return pltpu.make_async_remote_copy(
-                src_ref=slab.at[it], dst_ref=fold_in.at[it, pl.ds(pl.multiple_of(lon * ncols, SUB), ncols), :],
+                src_ref=slab.at[it, 1], dst_ref=fold_in.at[it, lon],
                 send_sem=fold_send.at[it, d], recv_sem=fold_recv.at[it, d],
                 device_id=dev(lax.rem(lon + d, nlon), lat), device_id_type=MESH,
             )
@@ -276,7 +275,7 @@
                 return c
 
             lax.fori_loop(1, nlon, start_fold, 0)
-            fold_in[it, pl.ds(pl.multiple_of(lon * ncols, SUB), ncols), :] = slab[it]
+            fold_in[it, lon] = slab[it, 1]
 
         lax.fori_loop(0, jnp.where(it == 0, 9, 8), conv, 0)
 
@@ -309,14 +308,19 @@
 
             lax.fori_loop(1, nlon, wait_fold, 0)
 
-            tops[...] = fold_in[it]
+            def spread(k, c):
+                tile = fold_in[it, k]
+                for r in range(R):
+                    tops[k, r] = tile if r == 0 else pltpu.roll(tile, LANES - 32 * r, 1)
+                return c
+
+            lax.fori_loop(0, nlon, spread, 0)
 
             def pick(i, c):
                 where = lax.rem(lon * ncols + i - width + nlon * ncols, nlon * ncols)
                 p = partner_ref[where]
                 col = lax.rem(p, ncols)
-                row = (p // ncols) * ncols + lax.rem(col, R) * SUB + col // R
-                D[pl.ds(i, 1), :] = tops[pl.ds(row, 1), :]
+                D[pl.ds(i, 1), :] = tops[p // ncols, lax.rem(col, R), pl.ds(col // R, 1), :]
                 return c
 
             lax.fori_loop(0, ncols + 2 * width, pick, 0)
@@ -329,24 +333,29 @@
                 G[1, p] = jnp.zeros((SUB, LANES), F32)
 
         small = lax.broadcasted_iota(jnp.int32, (SUB, LANES), 0)
-        for r in range(R):
-            G[0, width + r] = lat_in[it, 1, r * SUB : (r + 1) * SUB, :]
+        def piece(k, r):
+            return lat_in[it, k] if r == 0 else pltpu.roll(lat_in[it, k], LANES - 32 * r, 1)
+
+        own = [piece(1, r) for r in range(R)]
+        for r in range(R):
+            G[0, width + r] = own[r]
         for m in range(width):
             r = m + R - width
-            at = slice(r * SUB, (r + 1) * SUB)
-            G[0, m] = jnp.where(
-                small == 0, pltpu.roll(lat_in[it, 0, at, :], 1, 0), pltpu.roll(lat_in[it, 1, at, :], 1, 0)
-            )
-            at = slice(m * SUB, (m + 1) * SUB)
+            G[0, m] = jnp.where(small == 0, pltpu.roll(piece(0, r), 1, 0), pltpu.roll(own[r], 1, 0))
             G[0, R + width + m] = jnp.where(
-                small == SUB - 1,
-                pltpu.roll(lat_in[it, 2, at, :], SUB - 1, 0), pltpu.roll(lat_in[it, 1, at, :], SUB - 1, 0),
-            )
+                small == SUB - 1, pltpu.roll(piece(2, m), SUB - 1, 0), pltpu.roll(own[m], SUB - 1, 0)
+            )
+        for p in range(R + 2 * width):
+            G[1, p] = jnp.where(is_last, G[1, p], G[0, p])
 
         @pl.when(it == 0)
         def _():
             ocean_copy(0, right).wait()
             ocean_copy(1, left).wait()
+            for k in range(2):
+                for m in range(width):
+                    HL[k, m : m + 1, :] = ocean_in[0, 4 * k + m : 4 * k + m + 1, :]
+                    HL[k, 4 + m : 5 + m, :] = ocean_in[1, 4 * k + m : 4 * k + m + 1, :]
             row_correction([
                 jnp.concatenate([
                     jnp.broadcast_to(ocean_in[0, m : m + 1, :], (4, L)),
@@ -355,32 +364,39 @@
                 for m in range(width)
             ])
             add_rows(8, 0)
-            ghost(12, lambda k, p: G[k, p])
+            ghost(12)
             add_columns(8)
             for r in range(R):
                 rden[r] = 1.0 / (Y[8, r] + 1.0)
 
         head = lax.broadcasted_iota(jnp.int32, (4, L), 0) == 0
 
-        def local_rows(ref, m):
-            fq = factor * ref[it, 1, 4 + m : 5 + m, :]
-            at = 4 * m
-            field = ref[it, at // 8, at % 8 : at % 8 + 4, :]
-            return field * (1.0 - fq) + jnp.where(head, fq, 0.0)
+        for k in range(3):
+            for m in range(width):
+                HQ[k, m : m + 1, :] = low_in[it, m, 1 + k : 2 + k, :]
+                HQ[k, 4 + m : 5 + m, :] = high_in[it, m, 1 + k : 2 + k, :]
+        half = (HQ[0] - HQ[1]) * 0.5
+        tau = jnp.sqrt(half * half + HQ[2] * HQ[2] + 0.25)
+        over = jnp.maximum((tau + 0.35 * (HQ[0] + HQ[1])) * HL[1], 1.0)
+        HQ[3] = factor * (HL[0] * (1.0 - 1.0 / over))
+
+        def local_rows(ref, side_at, m):
+            fq = HQ[3, side_at + m : side_at + m + 1, :]
+            return ref[it, m] * (1.0 - fq) + jnp.where(head, fq, 0.0)
 
         row_correction([
-            jnp.concatenate([local_rows(low_in, m), local_rows(high_in, width - 1 - m)], axis=0)
+            jnp.concatenate([local_rows(low_in, 0, m), local_rows(high_in, 4, width - 1 - m)], axis=0)
             for m in range(width)
         ])
         for k in range(2):
             for p in range(R + 2 * width):
                 g = G[k, p]
-                G[k, p] = g + factor * pltpu.roll(g, LANES - 32, 1)
+                G[k, p] = g + factor * pltpu.roll(g, LANES - 16, 1)
         for f in range(4):
             for r in range(R):
                 Y[f, r] = Y[f, r] + factor * Y[4 + f, r]
             add_rows(f, f)
-            ghost(3 * f, lambda k, p: G[k, p])
+            ghost(3 * f)
             add_columns(f)
             for r in range(R):
                 state[f, r] = (0.5 * ocean[r]) * (Z[f, r] + factor * Z[4 + f, r] + Y[f, r] * rden[r])
@@ -413,17 +429,19 @@
             jax.ShapeDtypeStruct((ncols, nrows), F32),
             jax.ShapeDtypeStruct((ITERS, LANES), F32),
         ),
-        in_specs=[pl.BlockSpec(memory_space=pltpu.SMEM)] * 2 + [pl.BlockSpec(memory_space=pltpu.VMEM)] * 5,
+        in_specs=[pl.BlockSpec(memory_space=pltpu.SMEM)] * 2 + [pl.BlockSpec(memory_space=pltpu.HBM)] * 5,
         out_specs=(pl.BlockSpec(memory_space=pltpu.VMEM),) * 3,
         scratch_shapes=[
-            V(9, R, SUB, L), V(9, R, SUB, L), V(planes, SUB, L), V(R, SUB, L),
+            V(9, R, SUB, L), V(9, R, SUB, L), V(planes, SUB, L),
             V(3, R, SUB, L), V(R, SUB, L), V(R, SUB, L), V(R, SUB, L), V(R, SUB, L), V(4, R, SUB, L),
             V(width, SUB, L), V(2, planes, SUB, LANES), V(planes, SUB, LANES),
             V(-(-(ncols + 2 * width) // SUB) * SUB, LANES),
-            V(ITERS, 2, SUB, L), V(ITERS, 2, SUB, L), V(ITERS, 2, SUB, L), V(ITERS, 2, SUB, L),
+            V(ITERS, width, 4, L), V(ITERS, width, 4, L), V(ITERS, width, 4, L), V(ITERS, width, 4, L),
             V(2, SUB, L), V(2, SUB, L),
-            V(ITERS, ncols, LANES), V(ITERS, 3, ncols, LANES), V(ITERS, nlon * ncols, LANES),
-            V(ITERS, 2, LANES), V(ITERS, n, 2, LANES), V(9, L // LANES, ncols, LANES), V(nlon * ncols, LANES),
+            V(ITERS, 2, SUB, LANES), V(ITERS, 3, SUB, LANES), V(ITERS, nlon, SUB, LANES),
+            V(ITERS, 2, LANES), V(ITERS, n, 2, LANES), V(9, L // LANES, ncols, LANES), V(nlon, R, SUB, LANES),
+            V(4, SUB, L), V(2, SUB, L), V(3, ncols, nrows), V(3, ncols, nrows), V(ncols, nrows),
+            pltpu.VMEM((ncols, nrows), jnp.int32), pltpu.VMEM((ncols, nrows), jnp.int32), S(5),
             S(ITERS, 2), S(ITERS, 2), S(2), S(2), S(ITERS, 3), S(ITERS, 3), S(ITERS, nlon), S(ITERS, nlon),
             S(ITERS, n), S(ITERS, n),
         ],

time: 44.3 us -> 44.3 us (level)
  no operation moved by 1% of the time
where the time goes in v2:
time: 44.3 us; the launch traced here: 44 us
  Pallas kernels  35.2 us (79%)
  local copies, waits for them, and re-layouts  8.16 us (18%)
  between operations  0.66 us (1%)
    pallas_call x1, Pallas kernels, shards(): pl.pallas_call(functools.partial(kernel, nlon, nlat, nrows, R, L, side),...  35.2 us
    unnamed x16, local copies, waits for them, and re-layouts  7.53 us

profile of v2, /device:TPU:1, one launch (start us, length us, event | category | flops | bytes accessed | tf_op | source)
XLA Modules:
  0.0 44.0 jit_solution(83506819770218775)
XLA Ops:
  0.6 0.0 copy-start
  0.6 1.0 %copy-done = f32[3,32,1080]{2,1,0:T(8,128)S(1)} copy-done((f32[3,32,1080]{2,1,0:T(8,128)S(1)}, f32[3,32,1080]{2,1,0:T(8,128)}, u32[]{:S(2)}) %copy-start) | copy-done | bytes 414744
  1.6 0.0 copy-start.1
  1.6 1.0 %copy-done.1 = f32[3,32,1080]{2,1,0:T(8,128)S(1)} copy-done((f32[3,32,1080]{2,1,0:T(8,128)S(1)}, f32[3,32,1080]{2,1,0:T(8,128)}, u32[]{:S(2)}) %copy-start.1) | copy-done | bytes 414744
  2.7 0.0 copy-start.2
  2.7 0.9 %copy-done.2 = f32[32,1080]{1,0:T(8,128)S(1)} copy-done((f32[32,1080]{1,0:T(8,128)S(1)}, f32[32,1080]{1,0:T(8,128)}, u32[]{:S(2)}) %copy-start.2) | copy-done | bytes 138264
  3.6 0.0 copy-start.3
  3.6 0.9 %copy-done.3 = s32[32,1080]{1,0:T(8,128)S(1)} copy-done((s32[32,1080]{1,0:T(8,128)S(1)}, s32[32,1080]{1,0:T(8,128)}, u32[]{:S(2)}) %copy-start.3) | copy-done | bytes 138264
  4.5 0.0 copy-start.4
  4.5 0.9 %copy-done.4 = s32[32,1080]{1,0:T(8,128)S(1)} copy-done((s32[32,1080]{1,0:T(8,128)S(1)}, s32[32,1080]{1,0:T(8,128)}, u32[]{:S(2)}) %copy-start.4) | copy-done | bytes 138264
  5.4 0.0 copy-start.5
  5.4 0.7 %copy-done.5 = f32[7,7]{1,0:T(8,128)S(1)} copy-done((f32[7,7]{1,0:T(8,128)S(1)}, f32[7,7]{1,0:T(8,128)}, u32[]{:S(2)}) %copy-start.5) | copy-done | bytes 220
  6.1 0.0 copy-start.6
  6.1 0.7 %copy-done.6 = s32[256]{0:T(256)S(1)} copy-done((s32[256]{0:T(256)S(1)}, s32[256]{0:T(256)}, u32[]{:S(2)}) %copy-start.6) | copy-done | bytes 1048
  6.8 35.2 %shard_map.94 = (f32[3,32,1080]{2,1,0:T(8,128)S(1)}, f32[32,1080]{1,0:T(8,128)S(1)}, f32[3,128]{1,0:T(4,128)S(1)}) custom-call(f32[7,7]{1,0:T(8,128)S(1)} %copy-done.5, s32[256]{0:T(256)S(1)} %copy-done.6, f32[3,32,1080]{2,1,0:T(8,128)S(1)} %copy-done, f32[3,32,1080]{2,1,0:T(8,128)S(1)} %copy-done.1, f32[32,1080]{1,0:T(8,128)S(1)} %copy-done.2, ...), custom_call_target="tpu_custom_call" | custom-call | tf_op jit(solution)/shard_map/pallas_call | solution.py:425
  41.9 0.6 %slice_reduce_fusion = f32[3]{0:T(128)} fusion(f32[3,128]{1,0:T(4,128)S(1)} %get-tuple-element.8), kind=kLoop, calls=%fused_computation | loop fusion | bytes 24 | tf_op jit(solution)/shard_map/slice | solution.py:452
  42.6 0.8 %copy.12 = f32[3,32,1080]{2,1,0:T(8,128)} copy(f32[3,32,1080]{2,1,0:T(8,128)S(1)} %get-tuple-element.12) | data formatting | bytes 829440
  43.3 0.7 %copy.13 = f32[32,1080]{1,0:T(8,128)} copy(f32[32,1080]{1,0:T(8,128)S(1)} %get-tuple-element.13) | data formatting | bytes 276480
Async XLA Ops:
  0.6 1.0 %copy-start = (f32[3,32,1080]{2,1,0:T(8,128)S(1)}, f32[3,32,1080]{2,1,0:T(8,128)}, u32[]{:S(2)}) copy-start(f32[3,32,1080]{2,1,0:T(8,128)} %e_hbm.1) | copy-start | bytes 1244164
  1.6 1.0 %copy-start.1 = (f32[3,32,1080]{2,1,0:T(8,128)S(1)}, f32[3,32,1080]{2,1,0:T(8,128)}, u32[]{:S(2)}) copy-start(f32[3,32,1080]{2,1,0:T(8,128)} %s_hbm.1) | copy-start | bytes 1244164
  2.7 0.9 %copy-start.2 = (f32[32,1080]{1,0:T(8,128)S(1)}, f32[32,1080]{1,0:T(8,128)}, u32[]{:S(2)}) copy-start(f32[32,1080]{1,0:T(8,128)} %conc_hbm.1) | copy-start | bytes 414724
  3.6 0.9 %copy-start.3 = (s32[32,1080]{1,0:T(8,128)S(1)}, s32[32,1080]{1,0:T(8,128)}, u32[]{:S(2)}) copy-start(s32[32,1080]{1,0:T(8,128)} %class_hbm.1) | copy-start | bytes 414724
  4.5 0.9 %copy-start.4 = (s32[32,1080]{1,0:T(8,128)S(1)}, s32[32,1080]{1,0:T(8,128)}, u32[]{:S(2)}) copy-start(s32[32,1080]{1,0:T(8,128)} %mask_hbm.1) | copy-start | bytes 414724
  5.4 0.7 %copy-start.5 = (f32[7,7]{1,0:T(8,128)S(1)}, f32[7,7]{1,0:T(8,128)}, u32[]{:S(2)}) copy-start(f32[7,7]{1,0:T(8,128)} %w_ref.1) | copy-start | bytes 592
  6.1 0.7 %copy-start.6 = (s32[256]{0:T(256)S(1)}, s32[256]{0:T(256)}, u32[]{:S(2)}) copy-start(s32[256]{0:T(256)} %partner_ref.1) | copy-start | bytes 3076

commit v3 on v2

--- a/solution.py
+++ b/solution.py
@@ -295,6 +295,11 @@
         factor = 1.0 / (1.0 + 2.0 * mean)
         mean_ref[pl.ds(it, 1), :] = jnp.broadcast_to(mean, (1, LANES))
 
+        for f in range(4):
+            for r in range(R):
+                Y[f, r] = Y[f, r] + factor * Y[4 + f, r]
+                Z[f, r] = Z[f, r] + factor * Z[4 + f, r]
+
         up.wait()
         down.wait()
         for k in range(3):
@@ -393,13 +398,11 @@
                 g = G[k, p]
                 G[k, p] = g + factor * pltpu.roll(g, LANES - 16, 1)
         for f in range(4):
-            for r in range(R):
-                Y[f, r] = Y[f, r] + factor * Y[4 + f, r]
             add_rows(f, f)
             ghost(3 * f)
             add_columns(f)
             for r in range(R):
-                state[f, r] = (0.5 * ocean[r]) * (Z[f, r] + factor * Z[4 + f, r] + Y[f, r] * rden[r])
+                state[f, r] = (0.5 * ocean[r]) * (Z[f, r] + Y[f, r] * rden[r])
         return carry
 
     lax.fori_loop(0, ITERS, iteration, 0)
@@ -446,7 +449,7 @@
             S(ITERS, n), S(ITERS, n),
         ],
         compiler_params=pltpu.CompilerParams(
-            collective_id=0, has_side_effects=True, vmem_limit_bytes=48 * 1024 * 1024
+            collective_id=0, has_side_effects=True, vmem_limit_bytes=67043328
         ),
     )(kernel_weights, fold_partner, strain_rate, stress_start, concentration, cell_class, land_mask)
     return stress, damage, mean[:, 0]

time: 44.3 us -> 39.9 us (0.901)
  local copies, waits for them, and re-layouts: 8.16 us -> 3.8 us
    unnamed x16 -> x6, local copies, waits for them, and re-layouts: 7.53 us -> 3.17 us
where the time goes in v3:
time: 39.9 us; the launch traced here: 39.7 us
  Pallas kernels  35.3 us (88%)
  local copies, waits for them, and re-layouts  3.8 us (10%)
  between operations  0.65 us (2%)
    pallas_call x1, Pallas kernels, shards(): pl.pallas_call(functools.partial(kernel, nlon, nlat, nrows, R, L, side),...  35.3 us
    unnamed x6, local copies, waits for them, and re-layouts  3.17 us

profile of v3, /device:TPU:1, one launch (start us, length us, event | category | flops | bytes accessed | tf_op | source)
XLA Modules:
  0.0 39.7 jit_solution(18238487457085456778)
XLA Ops:
  0.6 35.3 %shard_map.94 = (f32[3,32,1080]{2,1,0:T(8,128)}, f32[32,1080]{1,0:T(8,128)}, f32[3,128]{1,0:T(4,128)}) custom-call(f32[7,7]{1,0:T(8,128)} %w_ref.1, s32[256]{0:T(256)} %partner_ref.1, f32[3,32,1080]{2,1,0:T(8,128)} %e_hbm.1, f32[3,32,1080]{2,1,0:T(8,128)} %s_hbm.1, f32[32,1080]{1,0:T(8,128)} %conc_hbm.1, s32[32,1080]{1,0:T(8,128)} %class_hbm.1, ...), custom_call_target="tpu_custom_call" | custom-call | tf_op jit(solution)/shard_map/pallas_call | solution.py:428
  35.9 0.0 copy-start.1
  35.9 0.7 %copy-done.1 = f32[3,128]{1,0:T(4,128)S(1)} copy-done((f32[3,128]{1,0:T(4,128)S(1)}, f32[3,128]{1,0:T(4,128)}, u32[]{:S(2)}) %copy-start.1) | copy-done | bytes 1560
  36.6 0.6 %slice_reduce_fusion = f32[3]{0:T(128)} fusion(f32[3,128]{1,0:T(4,128)S(1)} %copy-done.1), kind=kLoop, calls=%fused_computation | loop fusion | bytes 24 | tf_op jit(solution)/shard_map/slice | solution.py:455
  37.2 0.0 copy-start
  37.2 1.8 %copy.12 = f32[3,32,1080]{2,1,0:T(8,128)} copy(f32[3,32,1080]{2,1,0:T(8,128)} %get-tuple-element.12) | data formatting | bytes 829440
  39.1 0.0 copy-done
  39.1 0.7 %copy.13 = f32[32,1080]{1,0:T(8,128)} copy(f32[32,1080]{1,0:T(8,128)S(1)} %copy-done) | data formatting | bytes 276480
Async XLA Ops:
  35.9 0.7 %copy-start.1 = (f32[3,128]{1,0:T(4,128)S(1)}, f32[3,128]{1,0:T(4,128)}, u32[]{:S(2)}) copy-start(f32[3,128]{1,0:T(4,128)} %get-tuple-element.8) | copy-start | bytes 4612
  37.2 1.8 %copy-start = (f32[32,1080]{1,0:T(8,128)S(1)}, f32[32,1080]{1,0:T(8,128)}, u32[]{:S(2)}) copy-start(f32[32,1080]{1,0:T(8,128)} %get-tuple-element.13) | copy-start | bytes 414724

commit v4 on v3

--- a/solution.py
+++ b/solution.py
@@ -293,7 +293,7 @@
         sums = jnp.sum(total, axis=1, keepdims=True)
         mean = sums[0:1] / (sums[1:2] + 1.0)
         factor = 1.0 / (1.0 + 2.0 * mean)
-        mean_ref[pl.ds(it, 1), :] = jnp.broadcast_to(mean, (1, LANES))
+        mean_ref[it] = mean[0, 0]
 
         for f in range(4):
             for r in range(R):
@@ -328,7 +328,7 @@
                 D[pl.ds(i, 1), :] = tops[p // ncols, lax.rem(col, R), pl.ds(col // R, 1), :]
                 return c
 
-            lax.fori_loop(0, ncols + 2 * width, pick, 0)
+            lax.fori_loop(0, ncols + 2 * width, pick, 0, unroll=True)
             for p in range(R + 2 * width):
                 G[1, p] = D[pl.ds(p, SUB, stride=R), :]
 
@@ -428,12 +428,12 @@
     stress, damage, mean = pl.pallas_call(
         functools.partial(kernel, nlon, nlat, nrows, R, L, side),
         out_shape=(
-            jax.ShapeDtypeStruct((3, ncols, nrows), F32),
-            jax.ShapeDtypeStruct((ncols, nrows), F32),
-            jax.ShapeDtypeStruct((ITERS, LANES), F32),
+            pltpu.VMEM((3, ncols, nrows), F32),
+            pltpu.VMEM((ncols, nrows), F32),
+            jax.ShapeDtypeStruct((ITERS,), F32),
         ),
         in_specs=[pl.BlockSpec(memory_space=pltpu.SMEM)] * 2 + [pl.BlockSpec(memory_space=pltpu.HBM)] * 5,
-        out_specs=(pl.BlockSpec(memory_space=pltpu.VMEM),) * 3,
+        out_specs=(pl.BlockSpec(memory_space=pltpu.VMEM),) * 2 + (pl.BlockSpec(memory_space=pltpu.SMEM),),
         scratch_shapes=[
             V(9, R, SUB, L), V(9, R, SUB, L), V(planes, SUB, L),
             V(3, R, SUB, L), V(R, SUB, L), V(R, SUB, L), V(R, SUB, L), V(R, SUB, L), V(4, R, SUB, L),
@@ -449,10 +449,10 @@
             S(ITERS, n), S(ITERS, n),
         ],
         compiler_params=pltpu.CompilerParams(
-            collective_id=0, has_side_effects=True, vmem_limit_bytes=67043328
+            collective_id=0, has_side_effects=True, vmem_limit_bytes=67043328 - 1024 * 1024
         ),
     )(kernel_weights, fold_partner, strain_rate, stress_start, concentration, cell_class, land_mask)
-    return stress, damage, mean[:, 0]
+    return stress, damage, mean
 
 
 def solution(mesh):

time: 39.9 us -> 36.4 us (0.912)
  local copies, waits for them, and re-layouts: 3.8 us -> 1.94 us
  Pallas kernels: 35.3 us -> 33.6 us
    pallas_call x1, Pallas kernels: 35.3 us -> 33.6 us  [shards(): pl.pallas_call(functools.partial(kernel, nlon, nlat, nrows, R, L, side),...]
    unnamed x6 -> x5, local copies, waits for them, and re-layouts: 3.17 us -> 1.94 us
    slice x1 -> x0, local copies, waits for them, and re-layouts: 0.63 us -> none  [shards(): return (stress, damage, mean[:, 0])]
where the time goes in v4:
time: 36.4 us; the launch traced here: 36.2 us
  Pallas kernels  33.6 us (92%)
  local copies, waits for them, and re-layouts  1.94 us (5%)
  between operations  0.64 us (2%)
    pallas_call x1, Pallas kernels, shards(): pl.pallas_call(functools.partial(kernel, nlon, nlat, nrows, R, L, side),...  33.6 us
    unnamed x5, local copies, waits for them, and re-layouts  1.94 us

profile of v4, /device:TPU:1, one launch (start us, length us, event | category | flops | bytes accessed | tf_op | source)
XLA Modules:
  0.0 36.2 jit_solution(2428891332784446092)
XLA Ops:
  0.6 33.6 %shard_map.94 = (f32[3,32,1080]{2,1,0:T(8,128)S(1)}, f32[32,1080]{1,0:T(8,128)S(1)}, f32[3]{0:T(128)}) custom-call(f32[7,7]{1,0:T(8,128)} %w_ref.1, s32[256]{0:T(256)} %partner_ref.1, f32[3,32,1080]{2,1,0:T(8,128)} %e_hbm.1, f32[3,32,1080]{2,1,0:T(8,128)} %s_hbm.1, f32[32,1080]{1,0:T(8,128)} %conc_hbm.1, s32[32,1080]{1,0:T(8,128)} %class_hbm.1, ...), custom_call_target="tpu_custom_call" | custom-call | tf_op jit(solution)/shard_map/pallas_call | solution.py:428
  34.3 0.8 %copy.13 = f32[3,32,1080]{2,1,0:T(8,128)} copy(f32[3,32,1080]{2,1,0:T(8,128)S(1)} %get-tuple-element.3) | data formatting | bytes 829440
  35.0 0.0 copy-start
  35.0 0.7 %copy.14 = f32[32,1080]{1,0:T(8,128)} copy(f32[32,1080]{1,0:T(8,128)S(1)} %get-tuple-element.4) | data formatting | bytes 276480
  35.7 0.0 copy-done
  35.7 0.5 %copy.15 = f32[3]{0:T(128)} copy(f32[3]{0:T(128)S(1)} %copy-done) | data formatting | bytes 24
Async XLA Ops:
  35.0 0.7 %copy-start = (f32[3]{0:T(128)S(1)}, f32[3]{0:T(128)}, u32[]{:S(2)}) copy-start(f32[3]{0:T(128)} %get-tuple-element.11) | copy-start | bytes 40

commit v5 on v4

--- a/solution.py
+++ b/solution.py
@@ -277,7 +277,10 @@
             lax.fori_loop(1, nlon, start_fold, 0)
             fold_in[it, lon] = slab[it, 1]
 
-        lax.fori_loop(0, jnp.where(it == 0, 9, 8), conv, 0)
+        def early(j, c):
+            return conv(j + (j >= 3).astype(jnp.int32) + (j >= 6).astype(jnp.int32), c)
+
+        lax.fori_loop(0, jnp.where(it == 0, 7, 6), early, 0)
 
         def wait_stat(d, c):
             stat_copy(d).wait()
@@ -297,8 +300,11 @@
 
         for f in range(4):
             for r in range(R):
-                Y[f, r] = Y[f, r] + factor * Y[4 + f, r]
+                if f < 3:
+                    Y[f, r] = Y[f, r] + factor * Y[4 + f, r]
                 Z[f, r] = Z[f, r] + factor * Z[4 + f, r]
+
+        lax.fori_loop(3, 4, conv, 0)
 
         up.wait()
         down.wait()

time: 36.4 us -> 34.9 us (0.959)
  Pallas kernels: 33.6 us -> 32.1 us
    pallas_call x1, Pallas kernels: 33.6 us -> 32.1 us  [shards(): pl.pallas_call(functools.partial(kernel, nlon, nlat, nrows, R, L, side),...]
where the time goes in v5:
time: 34.9 us; the launch traced here: 34.7 us
  Pallas kernels  32.1 us (92%)
  local copies, waits for them, and re-layouts  1.94 us (6%)
  between operations  0.64 us (2%)
    pallas_call x1, Pallas kernels, shards(): pl.pallas_call(functools.partial(kernel, nlon, nlat, nrows, R, L, side),...  32.1 us
    unnamed x5, local copies, waits for them, and re-layouts  1.94 us

profile of v5, /device:TPU:1, one launch (start us, length us, event | category | flops | bytes accessed | tf_op | source)
XLA Modules:
  0.0 34.7 jit_solution(11428938267661811250)
XLA Ops:
  0.6 32.1 %shard_map.94 = (f32[3,32,1080]{2,1,0:T(8,128)S(1)}, f32[32,1080]{1,0:T(8,128)S(1)}, f32[3]{0:T(128)}) custom-call(f32[7,7]{1,0:T(8,128)} %w_ref.1, s32[256]{0:T(256)} %partner_ref.1, f32[3,32,1080]{2,1,0:T(8,128)} %e_hbm.1, f32[3,32,1080]{2,1,0:T(8,128)} %s_hbm.1, f32[32,1080]{1,0:T(8,128)} %conc_hbm.1, s32[32,1080]{1,0:T(8,128)} %class_hbm.1, ...), custom_call_target="tpu_custom_call" | custom-call | tf_op jit(solution)/shard_map/pallas_call | solution.py:434
  32.7 0.8 %copy.13 = f32[3,32,1080]{2,1,0:T(8,128)} copy(f32[3,32,1080]{2,1,0:T(8,128)S(1)} %get-tuple-element.3) | data formatting | bytes 829440
  33.5 0.0 copy-start
  33.5 0.7 %copy.14 = f32[32,1080]{1,0:T(8,128)} copy(f32[32,1080]{1,0:T(8,128)S(1)} %get-tuple-element.4) | data formatting | bytes 276480
  34.2 0.0 copy-done
  34.2 0.5 %copy.15 = f32[3]{0:T(128)} copy(f32[3]{0:T(128)S(1)} %copy-done) | data formatting | bytes 24
Async XLA Ops:
  33.5 0.7 %copy-start = (f32[3]{0:T(128)S(1)}, f32[3]{0:T(128)}, u32[]{:S(2)}) copy-start(f32[3]{0:T(128)} %get-tuple-element.11) | copy-start | bytes 40
